TPU v7x, 32 devices: a whole 2x2x4 slice. The times are simulated.
32 devices in a mesh: dom: 16 (over z, y, core), sub: 2 (over x).
Axes of the slice: x: 2, y: 2, z: 4, core: 2. Of those that a mesh axis runs over, the one named last changes fastest.
Arguments:
- dofs: float32 [9, 56, 512], P(None, None, ('dom', 'sub')), may hold values from -6 to 6
- stiffness: float32 [3, 56, 56], replicated, may hold values from -0.75 to 0.75
- projection: float32 [4, 21, 56], replicated, may hold values from -0.75 to 0.75
- star: float32 [3, 9, 9, 512], P(None, None, None, ('dom', 'sub')), may hold values from -1.25 to 1.25
- flux_minus: float32 [4, 9, 9, 512], P(None, None, None, ('dom', 'sub')), may hold values from -1 to 1
- flux_plus: float32 [4, 9, 9, 512], P(None, None, None, ('dom', 'sub')), may hold values from -1 to 1
- fault_flux: float32 [9, 9], replicated, may hold values from -2 to 2
- fault_faces: int32 [4, 512], P(None, ('dom', 'sub')), may hold values 0 or 1
- levels: int32 [512], P(('dom', 'sub')), may hold values from 0 to 1, as said below
- face_source: int32 [4, 512], P(None, ('dom', 'sub')), may hold values from 0 to 87
- send_source: int32 [128], P(('dom', 'sub')), may hold values from 0 to 63
Outputs:
- dofs_after: float32 [9, 56, 512], P(None, None, ('dom', 'sub'))
Inputs may be any that keep to these rules, and one draw needn't show every extreme that they name: `levels`: on every device at most 8 of its 16 elements have level 0, and some device has exactly 8.
All inputs are finite; a program needn't handle non-finite values. No bound on the sum of `fault_faces` on one device may be relied on, other than what follows from the above.
Results may differ from a plain program's by a relative error of at most 0.0001.
Values sent between devices are 32-bit elements; how exact they have to be, the bound alone decides.
A program may use at most 64 MiB of HBM per device.

v0:
```python
import math

import jax
import jax.numpy as jnp
from jax import lax
from jax.sharding import PartitionSpec as P

ORDER = 6


fine_step = 0.75
exact_reference = lax.Precision.HIGHEST


def padded(value, sides, width):
    for axis, dim in sides:
        count, length = (lax.axis_size(axis), value.shape[dim])
        up = [(i, (i + 1) % count) for i in range(count)]
        down = [(j, i) for i, j in up]
        last = lax.slice_in_dim(value, length - width, length, axis=dim)
        first = lax.slice_in_dim(value, 0, width, axis=dim)
        before = lax.ppermute(last, axis, up)
        after = lax.ppermute(first, axis, down)
        value = jnp.concatenate([before, value, after], axis=dim)
    return value


def taylor_weights(start_time, stop_time, term_count):
    return [
        (stop_time ** (term + 1) - start_time ** (term + 1)) / math.factorial(term + 1)
        for term in range(term_count)
    ]


def derivatives(state_now, stiffness, star_contribution):
    taylor_series = [state_now]
    for repeat in range(ORDER - 1):
        time_slopes = jnp.einsum(
            "dmn,wne->dwme", stiffness, taylor_series[-1], precision=exact_reference
        )
        taylor_series.append(
            jnp.einsum("usij,uifj->sfj", star_contribution, time_slopes, precision=exact_reference)
        )
    return jnp.stack(taylor_series)


def integrate(taylor_series, start_time, stop_time):
    quadrature_weights = jnp.array(
        taylor_weights(start_time, stop_time, taylor_series.shape[0]), jnp.float32
    )
    return jnp.einsum("h,hlui->lui", quadrature_weights, taylor_series, precision=exact_reference)


def face_values(field_state, projection):
    return jnp.einsum("bly,qyp->qlbp", projection, field_state, precision=exact_reference)


def advance(
    state_now,
    own_part,
    own_faces,
    beside,
    stiffness,
    projection,
    star_contribution,
    minus_part,
    coupling_part,
):
    incoming_flux = jnp.einsum(
        "dvwe,wne->dvne", star_contribution, own_part, precision=exact_reference
    )
    volume_term = jnp.einsum("utx,uytz->yxz", stiffness, incoming_flux, precision=exact_reference)
    flux_terms = jnp.einsum("fvwe,wjfe->vjfe", minus_part, own_faces, precision=exact_reference)
    flux_terms = flux_terms + jnp.einsum(
        "fvwe,wjfe->vjfe", coupling_part, beside, precision=exact_reference
    )
    surface_term = jnp.einsum("alz,qlad->qzd", projection, flux_terms, precision=exact_reference)
    return state_now + volume_term - surface_term


def exported(buffer):
    grouped = lax.all_gather(buffer, "sub", axis=2, tiled=True)
    stack_count, face_width, slot_count = grouped.shape
    neighbours_all = padded(
        grouped.reshape(stack_count, face_width, 1, slot_count), (("dom", 2),), 1
    )
    return neighbours_all.reshape(stack_count, face_width, 3 * slot_count)


def per_device(
    dofs,
    stiffness,
    projection,
    star,
    flux_minus,
    flux_plus,
    fault_flux,
    fault_faces,
    levels,
    face_source,
    send_source,
):
    var_count = dofs.shape[0]
    elem_count = dofs.shape[2]
    face_width = var_count * projection.shape[1]
    is_fine = levels == 0
    coupling = jnp.where(
        fault_faces[:, None, None, :] == 1, fault_flux[None, :, :, None], flux_plus
    )
    lookup = face_source.reshape(-1)

    def beside_values(local_faces, remote):
        source_table = jnp.concatenate(
            [local_faces.reshape(face_width, 4 * elem_count), remote], axis=1
        )
        return jnp.take(source_table, lookup, axis=1).reshape(var_count, -1, 4, elem_count)

    def put_columns(base, update):
        return jnp.where(is_fine, update, base)

    derivs = derivatives(dofs, stiffness, star)
    first_half = integrate(derivs, 0.0, fine_step)
    second_half = integrate(derivs, fine_step, 2.0 * fine_step)
    first_faces = face_values(first_half, projection)
    remote_first = exported(
        jnp.take(first_faces.reshape(face_width, 4 * elem_count), send_source, axis=1)[None]
    )[0]
    beside_first = beside_values(first_faces, remote_first)
    moved = advance(
        dofs,
        first_half,
        first_faces,
        beside_first,
        stiffness,
        projection,
        star,
        flux_minus,
        coupling,
    )
    state_one = put_columns(dofs, moved)
    fine_series = derivatives(state_one, stiffness, star)
    carried = put_columns(second_half, integrate(fine_series, 0.0, fine_step))
    carried_faces = face_values(carried, projection)
    remote_carried = exported(
        jnp.take(carried_faces.reshape(face_width, 4 * elem_count), send_source, axis=1)[None]
    )[0]
    beside_carried = beside_values(carried_faces, remote_carried)
    fine_new = advance(
        state_one,
        carried,
        carried_faces,
        beside_carried,
        stiffness,
        projection,
        star,
        flux_minus,
        coupling,
    )
    whole_step = first_half + second_half
    coarse_new = advance(
        dofs,
        whole_step,
        face_values(whole_step, projection),
        beside_first + beside_carried,
        stiffness,
        projection,
        star,
        flux_minus,
        coupling,
    )
    return put_columns(coarse_new, fine_new)


def solution(mesh):
    return jax.shard_map(
        per_device,
        mesh=mesh,
        in_specs=(
            P(None, None, ("dom", "sub")),
            P(),
            P(),
            P(None, None, None, ("dom", "sub")),
            P(None, None, None, ("dom", "sub")),
            P(None, None, None, ("dom", "sub")),
            P(),
            P(None, ("dom", "sub")),
            P(("dom", "sub")),
            P(None, ("dom", "sub")),
            P(("dom", "sub")),
        ),
        out_specs=P(None, None, ("dom", "sub")),
        check_vma=False,
    )
```

profile of v0, /device:TPU:0, one launch (start us, length us, event | category | flops | bytes accessed | tf_op | source)
XLA Modules:
  0.0 57.6 jit_solution(4794972899081313677)
XLA Ops:
  0.0 0.7 %compare_and_fusion.1 = pred[4]{0:T(512)(128)(4,1)S(1)} fusion(s32[4]{0:T(128)} %param.28), kind=kLoop, calls=%fused_computation.121 | loop fusion | flops 24 | bytes 20 | tf_op jit(solution)/shard_map/jit(_take)/and | solution.py:126
  0.8 1.2 %copy.67 = f32[3,9,9,16]{2,1,0,3:T(8,128)S(1)} copy(f32[3,9,9,16]{3,0,2,1:T(4,128)} %param.21) | data formatting | bytes 31104 | tf_op args[3]
  2.6 0.6 %bitcast_dynamic-update-slice_fusion.3 = (f32[6,9,56,16]{2,1,3,0:T(8,128)S(1)}, f32[16,56,9,1]{1,2,3,0:T(8,128)S(1)}) fusion(f32[6,9,56,16]{2,1,3,0:T(8,128)S(1)} %bitcast_dynamic-update-slice_fusion.4, f32[3,9,56,16]{2,1,0,3:T(8,128)S(1)} %convolution_bitcast_fusion.12, f32[3,9,9,16]{2,1,0,3:T(8,128)S(1)} %copy.67), kind=kOutput, calls=%fused_computation.48 | convolution fusion | flops 2612736 | bytes 1048576 | tf_op jit(solution)/shard_map/usij,uifj->sfj/dot_general | solution.py:42
  3.6 0.6 %bitcast_dynamic-update-slice_fusion.2 = (f32[6,9,56,16]{2,1,3,0:T(8,128)S(1)}, f32[16,56,9,1]{1,2,3,0:T(8,128)S(1)}) fusion(f32[6,9,56,16]{2,1,3,0:T(8,128)S(1)} %get-tuple-element.11, f32[3,9,56,16]{2,1,0,3:T(8,128)S(1)} %convolution_bitcast_fusion.11, f32[3,9,9,16]{2,1,0,3:T(8,128)S(1)} %copy.67), kind=kOutput, calls=%fused_computation.46 | convolution fusion | flops 2612736 | bytes 1048576 | tf_op jit(solution)/shard_map/usij,uifj->sfj/dot_general | solution.py:42
  4.7 0.6 %bitcast_dynamic-update-slice_fusion.1 = (f32[6,9,56,16]{2,1,3,0:T(8,128)S(1)}, f32[16,56,9,1]{1,2,3,0:T(8,128)S(1)}) fusion(f32[6,9,56,16]{2,1,3,0:T(8,128)S(1)} %get-tuple-element.13, f32[3,9,56,16]{2,1,0,3:T(8,128)S(1)} %convolution_bitcast_fusion.10, f32[3,9,9,16]{2,1,0,3:T(8,128)S(1)} %copy.67), kind=kOutput, calls=%fused_computation.44 | convolution fusion | flops 2612736 | bytes 1048576 | tf_op jit(solution)/shard_map/usij,uifj->sfj/dot_general | solution.py:42
  5.8 0.6 %bitcast_dynamic-update-slice_fusion = (f32[6,9,56,16]{2,1,3,0:T(8,128)S(1)}, f32[16,56,9,1]{1,2,3,0:T(8,128)S(1)}) fusion(f32[6,9,56,16]{2,1,3,0:T(8,128)S(1)} %get-tuple-element.15, f32[3,9,56,16]{2,1,0,3:T(8,128)S(1)} %convolution_bitcast_fusion.9, f32[3,9,9,16]{2,1,0,3:T(8,128)S(1)} %copy.67), kind=kOutput, calls=%fused_computation.42 | convolution fusion | flops 2612736 | bytes 1048576 | tf_op jit(solution)/shard_map/usij,uifj->sfj/dot_general | solution.py:42
  6.9 0.6 %fusion.3 = f32[6,9,56,16]{2,1,3,0:T(8,128)S(1)} fusion(f32[6,9,56,16]{2,1,3,0:T(8,128)S(1)} %get-tuple-element.17, f32[3,9,56,16]{2,1,0,3:T(8,128)S(1)} %convolution_bitcast_fusion.8, f32[3,9,9,16]{2,1,0,3:T(8,128)S(1)} %copy.67), kind=kOutput, calls=%fused_computation.28 | convolution fusion | flops 2612736 | bytes 917504 | tf_op jit(solution)/shard_map/usij,uifj->sfj/dot_general | solution.py:42
  7.5 0.9 %fusion.10 = f32[1,9,56,16]{2,0,3,1:T(1,128)S(1)} fusion(f32[6,1,1,1]{0,1,3,2:T(1,128)S(1)} %copy-done.7, f32[6,9,56,16]{2,1,3,0:T(8,128)S(1)} %fusion.3), kind=kOutput, calls=%fused_computation.35 | convolution fusion | flops 580608 | bytes 225816 | tf_op jit(solution)/shard_map/h,hlui->lui/dot_general | solution.py:51
  9.9 5.3 %all-gather.2 = f32[2,4,189]{2,1,0:T(4,128)S(1)} all-gather(f32[1,4,189]{2,1,0:T(4,128)S(1)} %select_bitcast_fusion.3), channel_id=2, replica_groups=mesh['dom'=16,'sub'=2] {'sub'}, dimensions={0}, use_global_device_ids=true | all-gather | bytes 9072 | tf_op jit(solution)/shard_map/all_gather | solution.py:82
  15.2 3.4 %collective-permute-start.1 = (f32[1,189,1,8]{1,3,2,0:T(8,128)S(1)}, f32[1,189,1,8]{1,3,2,0:T(8,128)S(1)}, u32[]{:S(2)}, u32[]{:S(2)}) collective-permute-start(f32[1,189,1,8]{1,3,2,0:T(8,128)S(1)} %bitcast.366), channel_id=1, source_target_pairs={{2,0},{4,2},{6,4},{8,6},{10,8},{12,10},{14,12},{16,14},{18,16},{20... | collective-permute-start | bytes 18152 | tf_op jit(solution)/shard_map/ppermute | solution.py:23
  18.8 0.6 %copy-done.11 = s32[4,16]{1,0:T(4,128)S(1)} copy-done((s32[4,16]{1,0:T(4,128)S(1)}, s32[4,16]{1,0:T(4,128)}, u32[]{:S(2)}) %copy-start.11) | copy-done | bytes 280
  20.1 0.9 %fusion.8 = f32[1,9,56,16]{2,0,3,1:T(1,128)S(1)} fusion(f32[6,1,1,1]{0,1,3,2:T(1,128)S(1)} %copy-done.12, f32[6,9,56,16]{2,1,3,0:T(8,128)S(1)} %fusion.3), kind=kOutput, calls=%fused_computation.33 | convolution fusion | flops 580608 | bytes 225816 | tf_op jit(solution)/shard_map/h,hlui->lui/dot_general | solution.py:51
  21.0 0.9 %fusion.43 = f32[4,16,21,9]{2,3,1,0:T(8,128)S(1)} fusion(f32[4,9,9,16]{2,1,3,0:T(8,128)S(1)} %copy.77, f32[9,21,4,16]{1,3,2,0:T(8,128)S(1)} %convolution_bitcast_fusion.15), kind=kOutput, calls=%fused_computation.75 | convolution fusion | flops 1306368 | bytes 117504 | tf_op jit(solution)/shard_map/fvwe,wjfe->vjfe/dot_general | solution.py:73
  22.3 0.9 %fusion.6 = f32[4,16,21,9]{2,3,1,0:T(8,128)S(1)} fusion(f32[4,9,9,16]{2,1,3,0:T(8,128)S(1)} %copy.77, f32[9,21,4,16]{1,3,2,0:T(8,128)S(1)} %convolution_bitcast_fusion.13), kind=kOutput, calls=%fused_computation.31 | convolution fusion | flops 1306368 | bytes 117504 | tf_op jit(solution)/shard_map/fvwe,wjfe->vjfe/dot_general | solution.py:73
  25.1 0.7 %gather_fusion.1 = f32[64,189]{1,0:T(8,128)S(1)} fusion(f32[189,88]{0,1:T(8,128)S(1)} %pad_maximum_fusion, s32[1024]{0:T(1024)S(1)} %pad_clamp_fusion), kind=kCustom, calls=%fused_computation.1.clone | custom fusion | bytes 97024 | tf_op jit(solution)/shard_map/jit(_take)/gather | solution.py:116
  26.2 1.2 %copy.82 = f32[9,21,4,16]{1,0,3,2:T(8,128)} copy(f32[9,21,4,16]{3,2,1,0:T(4,128)S(1)} %reshape.39) | data formatting | bytes 96768 | tf_op jit(solution)/shard_map/reshape | solution.py:116
  27.3 1.7 %fusion.2 = f32[9,21,4,16]{1,0,3,2:T(8,128)S(1)} fusion(f32[4,16,21,9]{2,3,1,0:T(8,128)S(1)} %fusion.43, f32[9,21,4,16]{1,0,3,2:T(8,128)} %copy.82, f32[4,9,9,16]{2,1,3,0:T(8,128)S(1)} %copy.83), kind=kOutput, calls=%fused_computation.9 | convolution fusion | flops 1318464 | bytes 165888 | tf_op jit(solution)/shard_map/fvwe,wjfe->vjfe/dot_general | solution.py:74
  30.2 0.6 %fusion.64 = f32[16,56,9,1]{1,2,3,0:T(8,128)S(1)} fusion(f32[3,9,56,16]{2,1,0,3:T(8,128)S(1)} %convolution_bitcast_fusion.6, f32[3,9,9,16]{2,1,0,3:T(8,128)S(1)} %copy.67), kind=kOutput, calls=%fused_computation.124 | convolution fusion | flops 2612736 | bytes 144576 | tf_op jit(solution)/shard_map/usij,uifj->sfj/dot_general | solution.py:42
  31.3 0.6 %fusion.65 = f32[16,56,9,1]{1,2,3,0:T(8,128)S(1)} fusion(f32[3,9,56,16]{2,1,0,3:T(8,128)S(1)} %convolution_bitcast_fusion.5, f32[3,9,9,16]{2,1,0,3:T(8,128)S(1)} %copy.67), kind=kOutput, calls=%fused_computation.125 | convolution fusion | flops 2612736 | bytes 144576 | tf_op jit(solution)/shard_map/usij,uifj->sfj/dot_general | solution.py:42
  32.3 0.6 %fusion.66 = f32[16,56,9,1]{1,2,3,0:T(8,128)S(1)} fusion(f32[3,9,56,16]{2,1,0,3:T(8,128)S(1)} %convolution_bitcast_fusion.4, f32[3,9,9,16]{2,1,0,3:T(8,128)S(1)} %copy.67), kind=kOutput, calls=%fused_computation.126 | convolution fusion | flops 2612736 | bytes 144576 | tf_op jit(solution)/shard_map/usij,uifj->sfj/dot_general | solution.py:42
  33.4 0.6 %fusion.67 = f32[16,56,9,1]{1,2,3,0:T(8,128)S(1)} fusion(f32[3,9,56,16]{2,1,0,3:T(8,128)S(1)} %convolution_bitcast_fusion.3, f32[3,9,9,16]{2,1,0,3:T(8,128)S(1)} %copy.67), kind=kOutput, calls=%fused_computation.127 | convolution fusion | flops 2612736 | bytes 144576 | tf_op jit(solution)/shard_map/usij,uifj->sfj/dot_general | solution.py:42
  34.5 0.6 %convolution_bitcast_fusion.16 = f32[16,56,9]{1,2,0:T(8,128)S(1)} fusion(f32[3,9,56,16]{2,1,0,3:T(8,128)S(1)} %convolution_bitcast_fusion.2, f32[3,9,9,16]{2,1,0,3:T(8,128)S(1)} %copy.67), kind=kOutput, calls=%fused_computation.26 | convolution fusion | flops 2612736 | bytes 144576 | tf_op jit(solution)/shard_map/usij,uifj->sfj/dot_general | solution.py:42
  35.3 1.0 %fusion.4 = f32[1,9,56,16]{2,0,3,1:T(1,128)S(1)} fusion(f32[6,1,1,1]{0,1,3,2:T(1,128)S(1)} %copy-done.7, f32[6,9,56,16]{2,3,1,0:T(8,128)S(1)} %bitcast_dynamic-update-slice_fusion.5), kind=kOutput, calls=%fused_computation.29 | convolution fusion | flops 580608 | bytes 225816 | tf_op jit(solution)/shard_map/h,hlui->lui/dot_general | solution.py:51
  36.8 0.9 %fusion.41 = f32[4,16,21,9]{2,3,1,0:T(8,128)S(1)} fusion(f32[4,9,9,16]{2,1,3,0:T(8,128)S(1)} %copy.77, f32[9,21,4,16]{1,3,2,0:T(8,128)S(1)} %convolution_bitcast_fusion.14), kind=kOutput, calls=%fused_computation.73 | convolution fusion | flops 1306368 | bytes 117504 | tf_op jit(solution)/shard_map/fvwe,wjfe->vjfe/dot_general | solution.py:73
  38.7 4.3 %all-gather.3 = f32[2,4,189]{2,1,0:T(4,128)S(1)} all-gather(f32[1,4,189]{2,1,0:T(4,128)S(1)} %select_bitcast_fusion.2), channel_id=3, replica_groups=mesh['dom'=16,'sub'=2] {'sub'}, dimensions={0}, use_global_device_ids=true | all-gather | bytes 9072 | tf_op jit(solution)/shard_map/all_gather | solution.py:82
  43.1 3.3 %collective-permute-start.3 = (f32[1,189,1,8]{1,3,2,0:T(8,128)S(1)}, f32[1,189,1,8]{1,3,2,0:T(8,128)S(1)}, u32[]{:S(2)}, u32[]{:S(2)}) collective-permute-start(f32[1,189,1,8]{1,3,2,0:T(8,128)S(1)} %bitcast.369), channel_id=1, source_target_pairs={{2,0},{4,2},{6,4},{8,6},{10,8},{12,10},{14,12},{16,14},{18,16},{20... | collective-permute-start | bytes 18152 | tf_op jit(solution)/shard_map/ppermute | solution.py:23
  47.8 1.1 %fusion.25 = f32[9,16,56,1]{2,0,3,1:T(8,128)} fusion(f32[3,9,56,16]{2,1,0,3:T(8,128)S(1)} %convolution_bitcast_fusion, f32[3,56,56]{2,1,0:T(8,128)S(1)} %copy-done), kind=kOutput, calls=%fused_computation.57 | convolution fusion | flops 16257024 | bytes 166656 | tf_op jit(solution)/shard_map/utx,uytz->yxz/dot_general | solution.py:72
  48.9 3.3 %collective-permute-done.2 = f32[1,189,1,8]{1,3,2,0:T(8,128)S(1)} collective-permute-done((f32[1,189,1,8]{1,3,2,0:T(8,128)S(1)}, f32[1,189,1,8]{1,3,2,0:T(8,128)S(1)}, u32[]{:S(2)}, u32[]{:S(2)}) %collective-permute-start.2) | collective-permute-done | bytes 6080 | tf_op jit(solution)/shard_map/ppermute | solution.py:22
  52.2 0.7 %gather_fusion.3 = f32[64,189]{1,0:T(8,128)S(1)} fusion(f32[189,88]{0,1:T(8,128)S(1)} %pad_maximum_fusion.1, s32[1024]{0:T(1024)S(1)} %pad_clamp_fusion), kind=kCustom, calls=%fused_computation.3.clone | custom fusion | bytes 97024 | tf_op jit(solution)/shard_map/jit(_take)/gather | solution.py:116
  53.8 0.6 %fusion.1 = f32[9,21,4,16]{1,0,3,2:T(8,128)S(1)} fusion(f32[4,16,21,9]{2,3,1,0:T(8,128)S(1)} %fusion.41, f32[9,21,4,16]{1,0,3,2:T(8,128)S(1)} %copy.111, f32[4,9,9,16]{2,1,3,0:T(8,128)S(1)} %copy.83), kind=kOutput, calls=%fused_computation.7 | convolution fusion | flops 1318464 | bytes 165888 | tf_op jit(solution)/shard_map/fvwe,wjfe->vjfe/dot_general | solution.py:74
  55.4 0.6 %fusion = f32[9,21,4,16]{1,0,3,2:T(8,128)S(1)} fusion(f32[4,16,21,9]{2,3,1,0:T(8,128)S(1)} %fusion.6, f32[9,21,4,16]{1,0,3,2:T(8,128)S(1)} %copy.121, f32[4,9,9,16]{2,1,3,0:T(8,128)S(1)} %copy.83), kind=kOutput, calls=%fused_computation.5 | convolution fusion | flops 1318464 | bytes 165888 | tf_op jit(solution)/shard_map/fvwe,wjfe->vjfe/dot_general | solution.py:74
  56.9 0.7 %fusion.45 = f32[9,56,16]{1,2,0:T(8,128)} fusion(f32[9,56,16]{1,2,0:T(8,128)S(1)} %copy-done.2, f32[9,56,16]{1,2,0:T(8,128)S(1)} %get-tuple-element.8, f32[9,16,56,1]{2,0,1,3:T(8,128)S(1)} %fusion.49, f32[9,16,56,1]{2,0,3,1:T(8,128)S(1)} %copy-done.3, f32[9,16,56,1]{2,0,1,3:T(8,128)S(1)} %fusion.51, f32[9,16,56,1]{2,0,3,1:T(8,128)S(1)} %fusion.27, ...), kind=kLoop, calls=%fused_computation.79 | loop fusion | flops 40320 | bytes 225808 | tf_op jit(solution)/shard_map/jit(_where)/select_n | solution.py:119
  (97 shorter events, 16.2 us)
Async XLA Ops:
  0.0 2.1 %copy-start = (f32[3,56,56]{2,1,0:T(8,128)S(1)}, f32[3,56,56]{2,1,0:T(8,128)}, u32[]{:S(2)}) copy-start(f32[3,56,56]{2,1,0:T(8,128)} %param.19) | copy-start | bytes 112900
  0.0 0.7 %copy-start.13 = (s32[4]{0:T(128)S(1)}, s32[4]{0:T(128)}, u32[]{:S(2)}) copy-start(s32[4]{0:T(128)} %param.28) | copy-start | bytes 52
  0.7 9.1 %copy-start.8 = (pred[4]{0:T(512)(128)(4,1)}, pred[4]{0:T(512)(128)(4,1)S(1)}, u32[]{:S(2)}) copy-start(pred[4]{0:T(512)(128)(4,1)S(1)} %compare_and_fusion.1) | copy-start | bytes 16
  0.8 1.2 %copy-start.2 = (f32[9,56,16]{1,2,0:T(8,128)S(1)}, f32[9,56,16]{1,2,0:T(8,128)}, u32[]{:S(2)}) copy-start(f32[9,56,16]{1,2,0:T(8,128)} %param.18) | copy-start | bytes 96772
  6.9 0.7 %copy-start.7 = (f32[6,1,1,1]{0,1,3,2:T(1,128)S(1)}, f32[6,1,1,1]{0,1,3,2:T(1,128)}, u32[]{:S(2)}) copy-start(f32[6,1,1,1]{0,1,3,2:T(1,128)} %constant.38) | copy-start | bytes 76
  7.5 0.9 %copy-start.1 = (f32[4,21,56]{2,0,1:T(4,128)S(1)}, f32[4,21,56]{2,0,1:T(4,128)}, u32[]{:S(2)}) copy-start(f32[4,21,56]{2,0,1:T(4,128)} %param.20) | copy-start | bytes 56452
  9.2 9.4 %copy-start.10 = (s32[4,16]{1,0:T(4,128)S(1)}, s32[4,16]{1,0:T(4,128)}, u32[]{:S(2)}) copy-start(s32[4,16]{1,0:T(4,128)} %param.27) | copy-start | bytes 772
  9.2 9.5 %copy-start.14 = (s32[16]{0:T(128)S(1)}, s32[16]{0:T(128)}, u32[]{:S(2)}) copy-start(s32[16]{0:T(128)} %param.26) | copy-start | bytes 196
  9.3 10.2 %copy-start.4 = (f32[4,9,9,16]{3,0,2,1:T(4,128)S(1)}, f32[4,9,9,16]{3,0,2,1:T(4,128)}, u32[]{:S(2)}) copy-start(f32[4,9,9,16]{3,0,2,1:T(4,128)} %param.22) | copy-start | bytes 62212
  15.2 9.9 %collective-permute-start.1 = (f32[1,189,1,8]{1,3,2,0:T(8,128)S(1)}, f32[1,189,1,8]{1,3,2,0:T(8,128)S(1)}, u32[]{:S(2)}, u32[]{:S(2)}) collective-permute-start(f32[1,189,1,8]{1,3,2,0:T(8,128)S(1)} %bitcast.366), channel_id=1, source_target_pairs={{2,0},{4,2},{6,4},{8,6},{10,8},{12,10},{14,12},{16,14},{18,16},{20... | collective-permute-start | bytes 18152 | tf_op jit(solution)/shard_map/ppermute | solution.py:23
  18.6 6.4 %collective-permute-start = (f32[1,189,1,8]{1,3,2,0:T(8,128)S(1)}, f32[1,189,1,8]{1,3,2,0:T(8,128)S(1)}, u32[]{:S(2)}, u32[]{:S(2)}) collective-permute-start(f32[1,189,1,8]{1,3,2,0:T(8,128)S(1)} %bitcast.367), channel_id=1, source_target_pairs={{0,2},{2,4},{4,6},{6,8},{8,10},{10,12},{12,14},{14,16},{16,18},{18... | collective-permute-start | bytes 18152 | tf_op jit(solution)/shard_map/ppermute | solution.py:22
  18.7 0.7 %copy-start.11 = (s32[4,16]{1,0:T(4,128)S(1)}, s32[4,16]{1,0:T(4,128)}, u32[]{:S(2)}) copy-start(s32[4,16]{1,0:T(4,128)} %param.25) | copy-start | bytes 772
  19.4 0.7 %copy-start.12 = (f32[6,1,1,1]{0,1,3,2:T(1,128)S(1)}, f32[6,1,1,1]{0,1,3,2:T(1,128)}, u32[]{:S(2)}) copy-start(f32[6,1,1,1]{0,1,3,2:T(1,128)} %constant.39) | copy-start | bytes 76
  23.6 0.9 %copy-start.5 = (f32[4,9,9,16]{3,0,2,1:T(4,128)S(1)}, f32[4,9,9,16]{3,0,2,1:T(4,128)}, u32[]{:S(2)}) copy-start(f32[4,9,9,16]{3,0,2,1:T(4,128)} %param.23) | copy-start | bytes 62212
  23.6 0.9 %copy-start.6 = (f32[9,9]{1,0:T(8,128)S(1)}, f32[9,9]{1,0:T(8,128)}, u32[]{:S(2)}) copy-start(f32[9,9]{1,0:T(8,128)} %param.24) | copy-start | bytes 976
  38.0 0.7 %copy-start.9 = (pred[4]{0:T(512)(128)(4,1)S(1)}, pred[4]{0:T(512)(128)(4,1)}, u32[]{:S(2)}) copy-start(pred[4]{0:T(512)(128)(4,1)} %copy-done.8) | copy-start | bytes 16
  43.1 5.8 %collective-permute-start.3 = (f32[1,189,1,8]{1,3,2,0:T(8,128)S(1)}, f32[1,189,1,8]{1,3,2,0:T(8,128)S(1)}, u32[]{:S(2)}, u32[]{:S(2)}) collective-permute-start(f32[1,189,1,8]{1,3,2,0:T(8,128)S(1)} %bitcast.369), channel_id=1, source_target_pairs={{2,0},{4,2},{6,4},{8,6},{10,8},{12,10},{14,12},{16,14},{18,16},{20... | collective-permute-start | bytes 18152 | tf_op jit(solution)/shard_map/ppermute | solution.py:23
  46.4 5.8 %collective-permute-start.2 = (f32[1,189,1,8]{1,3,2,0:T(8,128)S(1)}, f32[1,189,1,8]{1,3,2,0:T(8,128)S(1)}, u32[]{:S(2)}, u32[]{:S(2)}) collective-permute-start(f32[1,189,1,8]{1,3,2,0:T(8,128)S(1)} %bitcast.370), channel_id=1, source_target_pairs={{0,2},{2,4},{4,6},{6,8},{8,10},{10,12},{12,14},{14,16},{16,18},{18... | collective-permute-start | bytes 18152 | tf_op jit(solution)/shard_map/ppermute | solution.py:22
  56.0 0.9 %copy-start.3 = (f32[9,16,56,1]{2,0,3,1:T(8,128)S(1)}, f32[9,16,56,1]{2,0,3,1:T(8,128)}, u32[]{:S(2)}) copy-start(f32[9,16,56,1]{2,0,3,1:T(8,128)} %fusion.25) | copy-start | bytes 96772
where the time goes:
time: 57.9 us; the launch traced here: 57.6 us
  matrix products  25.4 us (44%)
  local copies, waits for them, and re-layouts  9.69 us (17%)
  blocking collectives  9.62 us (17%)
  starting transfers between devices  6.76 us (12%)
  waiting for transfers between devices  3.34 us (6%)
  other arithmetic  2.23 us (4%)
  between operations  0.58 us (1%)
    all_gather x2, blocking collectives, exported(): grouped = lax.all_gather(buffer, 'sub', axis=2, tiled=True)  9.62 us
    ppermute x2, starting transfers between devices, padded(): after = lax.ppermute(first, axis, down)  6.76 us
    dot_general x10, matrix products, derivatives(): jnp.einsum('usij,uifj->sfj', star_contribution, time_slopes, precision=ex...  6.03 us
    dot_general x10, matrix products, derivatives(): jnp.einsum('dmn,wne->dwme', stiffness, taylor_series[-1], precision=exact...  4.75 us
    unnamed x39, local copies, waits for them, and re-layouts  3.62 us
    ppermute x2, waiting for transfers between devices, padded(): before = lax.ppermute(last, axis, up)  3.33 us
    dot_general x3, matrix products, advance(): jnp.einsum('fvwe,wjfe->vjfe', coupling_part, beside, precision=exact_refe...  2.94 us
    dot_general x3, matrix products, integrate(): jnp.einsum('h,hlui->lui', quadrature_weights, taylor_series, precision=ex...  2.74 us
  transfers between devices with their start and end apart: 4, of which 1 were waited for; matrix products, arithmetic and copies ran while one was open for 13% of the time, Pallas kernels for 0%

commit v1 on v0

v1 whole, which is shorter than its diff:
```python
import functools
import math

import jax
import jax.numpy as jnp
from jax import lax
from jax.experimental import pallas as pl
from jax.experimental.pallas import tpu as pltpu
from jax.sharding import PartitionSpec as P

MESH = pl.DeviceIdType.MESH
ORDER = 6
fine_step = 0.75
F32 = jnp.float32
BF16 = jnp.bfloat16


def taylor_weights(start_time, stop_time, term_count):
    return [
        (stop_time ** (term + 1) - start_time ** (term + 1)) / math.factorial(term + 1)
        for term in range(term_count)
    ]


def up_to(value, step):
    return -(-value // step) * step


def dot(a, b):
    return jnp.dot(a, b, preferred_element_type=F32)


def split(value):
    high = value.astype(BF16)
    return high, (value - high.astype(F32)).astype(BF16)


def stacked(value):
    return jnp.concatenate(split(value), axis=0)


def halves(product):
    rows = product.shape[0] // 2
    return product[:rows] + product[rows:]


def left_product(left_both, right):
    high, low = split(right)
    rows = left_both.shape[0] // 2
    return halves(dot(left_both, high)) + dot(left_both[:rows], low)


def right_product(left_both, right_high, right_low):
    rows = left_both.shape[0] // 2
    return halves(dot(left_both, right_high)) + dot(left_both[:rows], right_low)


def kernel(
    sizes,
    dofs,
    stiffness,
    projection,
    star,
    flux_minus,
    flux_plus,
    fault_flux,
    fault_faces,
    levels,
    face_source,
    send_source,
    out,
    rows_ref,
    ints,
    block_high,
    block_low,
    picks,
    flat,
    small,
    state,
    export,
    received,
    send_sem,
    recv_sem,
):
    n_dom, n_sub = sizes
    var_count, modes, elems = dofs.shape
    dims = stiffness.shape[0]
    faces, face_modes = projection.shape[0], projection.shape[1]
    slots = send_source.shape[1]
    lanes = var_count * elems
    m_pad = up_to(modes, 16)
    j_pad = up_to(face_modes, 16)
    j_sent = export.shape[1]
    per_table = elems // slots
    sources = 3 * n_sub
    tables = -(-sources // per_table)

    me_dom, me_sub = lax.axis_index("dom"), lax.axis_index("sub")
    partners = []
    for delta in (-1, 0, 1):
        for turn in range(n_sub):
            if delta or turn:
                partners.append(
                    (
                        (
                            lax.rem(me_dom + delta + n_dom, n_dom),
                            lax.rem(me_sub + turn, n_sub),
                        ),
                        (1 - delta) * n_sub + me_sub,
                    )
                )
    barrier = pltpu.get_barrier_semaphore()
    for target, _ in partners:
        pl.semaphore_signal(barrier, inc=1, device_id=target, device_id_type=MESH)

    state[...] = jnp.zeros_like(state)
    for v in range(var_count):
        state[0:modes, v * elems : (v + 1) * elems] = dofs[v]

    for d in range(dims):
        for v in range(var_count):
            rows_ref[d, 0:var_count, v * elems : (v + 1) * elems] = star[d, v]

    small[...] = jnp.zeros_like(small)
    for d in range(dims):
        small[0:modes, d * m_pad : d * m_pad + modes] = stiffness[d]
    forward = stacked(small[0:m_pad, 0 : dims * m_pad])

    mask = (
        lax.broadcasted_iota(jnp.int32, (elems, lanes), 1) % elems
        == lax.broadcasted_iota(jnp.int32, (elems, lanes), 0)
    )

    def spread(i):
        for w in range(var_count):
            row = rows_ref[i, w : w + 1, :]
            high = row.astype(BF16).astype(F32)
            low = row - high
            at = slice(w * elems, (w + 1) * elems)
            block_high[i, at, :] = jnp.where(mask, high, 0.0).astype(BF16)
            block_low[i, at, :] = jnp.where(mask, low, 0.0).astype(BF16)

    for d in range(dims):
        spread(d)

    def turned(value):
        both = stacked(value)
        return [
            right_product(both, block_high[d], block_low[d]) for d in range(dims)
        ]

    def series(value, weight_sets):
        totals = [weights[0] * value for weights in weight_sets]
        for term in range(1, ORDER):
            value = left_product(forward, jnp.concatenate(turned(value), axis=0))
            totals = [
                total + weights[term] * value
                for total, weights in zip(totals, weight_sets)
            ]
        return totals

    first_weights = taylor_weights(0.0, fine_step, ORDER)
    second_weights = taylor_weights(fine_step, 2.0 * fine_step, ORDER)
    first_half, second_half = series(state[...], (first_weights, second_weights))

    flat[...] = jnp.zeros_like(flat)
    for d in range(dims):
        flat[d * m_pad : d * m_pad + modes, 0:modes] = stiffness[d]
    base = dims * m_pad
    for f in range(faces):
        flat[base + f * j_pad : base + f * j_pad + face_modes, 0:modes] = -projection[f]
    base_fault = base + faces * j_pad
    flat[base_fault : base_fault + var_count, 0:var_count] = fault_flux[...]
    project = stacked(-flat[base : base + faces * j_pad, 0:m_pad])
    flipped = jnp.transpose(flat[...])
    back = stacked(flipped[0:m_pad, 0:base_fault])

    for i in range(per_table):
        ints[9:10, i * slots : (i + 1) * slots] = send_source[...]
    send_row = ints[9:10, 0:elems]
    for v in range(var_count):
        at = slice(v * elems, (v + 1) * elems)
        ints[0:faces, at] = face_source[...]
        ints[4 : 4 + faces, at] = fault_faces[...]
        ints[8:9, at] = levels[...]
        ints[9:10, at] = send_row

    row_id = lax.broadcasted_iota(jnp.int32, (lanes, lanes), 0)
    lane_id = lax.broadcasted_iota(jnp.int32, (lanes, lanes), 1)
    key = jnp.where(row_id // elems == lane_id // elems, row_id % elems, -(2**20))

    def pick(row, f):
        return jnp.where(key == ints[row : row + 1, :] - f * elems, 1.0, 0.0).astype(BF16)

    def face_halves(value):
        both = stacked(left_product(project, value))
        count = faces * j_pad
        return [
            jnp.concatenate(
                [
                    both[f * j_pad : (f + 1) * j_pad],
                    both[count + f * j_pad : count + (f + 1) * j_pad],
                ],
                axis=0,
            )
            for f in range(faces)
        ]

    def total_of(parts):
        return functools.reduce(lambda a, b: a + b, parts)

    send_picks = [pick(9, f) for f in range(faces)]
    own_slot = n_sub + me_sub

    def launch(phase, face_parts):
        block = halves(
            total_of([dot(part, one) for part, one in zip(face_parts, send_picks)])
        )[0:j_sent]
        export[phase] = block
        copies = []
        for i, (target, slot) in enumerate(partners):
            copy = pltpu.make_async_remote_copy(
                src_ref=export.at[phase],
                dst_ref=received.at[phase, slot],
                send_sem=send_sem.at[phase, i],
                recv_sem=recv_sem.at[phase, i],
                device_id=target,
                device_id_type=MESH,
            )
            copy.start()
            copies.append(copy)
        received[phase, own_slot] = block
        return copies

    def local_part(value, face_parts):
        volume = turned(value)
        own = [
            right_product(face_parts[f], block_high[dims + f], block_low[dims + f])
            for f in range(faces)
        ]
        beside = [
            total_of([dot(face_parts[g], picks[g, f]) for g in range(faces)])
            for f in range(faces)
        ]
        return volume, own, beside

    table_lane = lax.broadcasted_iota(jnp.int32, (j_sent, lanes), 1) % elems // slots

    def finish(phase, copies, parts):
        volume, own, beside = parts
        for copy in copies:
            copy.wait()
        table_parts = []
        for t in range(tables):
            table = jnp.zeros((j_sent, lanes), F32)
            for i in range(min(per_table, sources - t * per_table)):
                table = jnp.where(
                    table_lane == i, received[phase, t * per_table + i], table
                )
            if j_pad > j_sent:
                table = jnp.concatenate(
                    [table, jnp.zeros((j_pad - j_sent, lanes), F32)], axis=0
                )
            table_parts.append(stacked(table))
        flux = []
        for f in range(faces):
            gathered = halves(
                beside[f]
                + total_of(
                    [dot(table_parts[t], picks[faces + t, f]) for t in range(tables)]
                )
            )
            at = dims + faces + f
            flux.append(
                own[f] + right_product(stacked(gathered), block_high[at], block_low[at])
            )
        return left_product(back, jnp.concatenate(volume + flux, axis=0))

    face_parts = face_halves(first_half)
    pl.semaphore_wait(barrier, len(partners))
    copies = launch(0, face_parts)

    for v in range(var_count):
        at = slice(v * elems, (v + 1) * elems)
        fault_column = flipped[0:var_count, base_fault + v : base_fault + v + 1]
        for f in range(faces):
            rows_ref[dims + f, 0:var_count, at] = flux_minus[f, v]
            rows_ref[dims + faces + f, 0:var_count, at] = jnp.where(
                fault_faces[f : f + 1, :] == 1, fault_column, flux_plus[f, v]
            )
    for i in range(dims, dims + 2 * faces):
        spread(i)
    for f in range(faces):
        for g in range(faces + tables):
            picks[g, f] = pick(f, g)

    parts = local_part(first_half, face_parts)
    moved = state[...] + finish(0, copies, parts)
    (fine_half,) = series(moved, (first_weights,))
    carried = jnp.where(ints[8:9, :] == 0, fine_half, second_half)
    face_parts = face_halves(carried)
    copies = launch(1, face_parts)
    parts = local_part(carried, face_parts)
    result = moved + finish(1, copies, parts)
    for v in range(var_count):
        out[v] = result[0:modes, v * elems : (v + 1) * elems]


def solution(mesh):
    n_dom, n_sub = mesh.shape["dom"], mesh.shape["sub"]

    def per_device(
        dofs,
        stiffness,
        projection,
        star,
        flux_minus,
        flux_plus,
        fault_flux,
        fault_faces,
        levels,
        face_source,
        send_source,
    ):
        var_count, modes, elems = dofs.shape
        dims = stiffness.shape[0]
        faces, face_modes = projection.shape[0], projection.shape[1]
        slots = send_source.shape[0]
        lanes = var_count * elems
        m_pad, j_pad = up_to(modes, 16), up_to(face_modes, 16)
        j_sent = up_to(face_modes, 8)
        sources = 3 * n_sub
        tables = -(-sources // (elems // slots))
        blocks = dims + 2 * faces
        flat_rows = up_to(dims * m_pad + faces * j_pad + var_count, 128)
        vmem = pl.BlockSpec(memory_space=pltpu.VMEM)
        return pl.pallas_call(
            functools.partial(kernel, (n_dom, n_sub)),
            out_shape=jax.ShapeDtypeStruct(dofs.shape, F32),
            in_specs=[vmem] * 11,
            out_specs=vmem,
            scratch_shapes=[
                pltpu.VMEM((blocks, up_to(var_count, 8), lanes), F32),
                pltpu.VMEM((16, lanes), jnp.int32),
                pltpu.VMEM((blocks, lanes, lanes), BF16),
                pltpu.VMEM((blocks, lanes, lanes), BF16),
                pltpu.VMEM((faces + tables, faces, lanes, lanes), BF16),
                pltpu.VMEM((flat_rows, 128), F32),
                pltpu.VMEM((m_pad, up_to(dims * m_pad, 128)), F32),
                pltpu.VMEM((m_pad, lanes), F32),
                pltpu.VMEM((2, j_sent, lanes), F32),
                pltpu.VMEM((2, sources, j_sent, lanes), F32),
                pltpu.SemaphoreType.DMA((2, sources - 1)),
                pltpu.SemaphoreType.DMA((2, sources - 1)),
            ],
            compiler_params=pltpu.CompilerParams(
                collective_id=0,
                has_side_effects=True,
                vmem_limit_bytes=48 * 1024 * 1024,
            ),
            name="window",
        )(
            dofs,
            stiffness,
            projection,
            star,
            flux_minus,
            flux_plus,
            fault_flux,
            fault_faces,
            levels.reshape(1, -1),
            face_source,
            send_source.reshape(1, -1),
        )

    return jax.shard_map(
        per_device,
        mesh=mesh,
        in_specs=(
            P(None, None, ("dom", "sub")),
            P(),
            P(),
            P(None, None, None, ("dom", "sub")),
            P(None, None, None, ("dom", "sub")),
            P(None, None, None, ("dom", "sub")),
            P(),
            P(None, ("dom", "sub")),
            P(("dom", "sub")),
            P(None, ("dom", "sub")),
            P(("dom", "sub")),
        ),
        out_specs=P(None, None, ("dom", "sub")),
        check_vma=False,
    )
```

time: 57.9 us -> 25.3 us (0.44)
  matrix products: 25.4 us -> 0 us
  Pallas kernels: 0 us -> 19.8 us
  blocking collectives: 9.62 us -> 0 us
  starting transfers between devices: 6.76 us -> 0 us
  local copies, waits for them, and re-layouts: 9.69 us -> 5.21 us
  waiting for transfers between devices: 3.34 us -> 0 us
  other arithmetic: 2.23 us -> 0 us
    dot_general x41 -> x0, matrix products: 25.4 us -> none  [the longest x10 6.03 us: derivatives(): jnp.einsum('usij,uifj->sfj', star_contribution, time_slopes, precision=ex...]
    pallas_call x0 -> x1, Pallas kernels: none -> 19.8 us  [per_device(): pl.pallas_call(functools.partial(kernel, (n_dom, n_sub)), out_shape=jax.S...]
    all_gather x2 -> x0, blocking collectives: 9.62 us -> none  [exported(): grouped = lax.all_gather(buffer, 'sub', axis=2, tiled=True)]
    ppermute x4 -> x0, starting transfers between devices: 6.76 us -> none  [the longest x2 6.76 us: padded(): after = lax.ppermute(first, axis, down)]
    ppermute x4 -> x0, waiting for transfers between devices: 3.34 us -> none  [the longest x2 3.33 us: padded(): before = lax.ppermute(last, axis, up)]
    gather x4 -> x0, local copies, waits for them, and re-layouts: 2.43 us -> none  [the longest x2 1.31 us: beside_values(): jnp.take(source_table, lookup, axis=1).reshape(var_count, -1, 4, elem_count)]
    reshape x7 -> x0, local copies, waits for them, and re-layouts: 2.35 us -> none  [the longest x4 1.96 us: beside_values(): jnp.take(source_table, lookup, axis=1).reshape(var_count, -1, 4, elem_count)]
    select_n x7 -> x0, other arithmetic: 1.11 us -> none  [the longest x2 0.8 us: put_columns(): return jnp.where(is_fine, update, base)]
  transfers between devices with their start and end apart: 4 -> 0, of which waited for: 1 -> 0; matrix products, arithmetic and copies ran while one was open for 13% -> 0% of each run, Pallas kernels for 0% -> 0%
where the time goes in v1:
time: 25.3 us; the launch traced here: 25.1 us
  Pallas kernels  19.8 us (78%)
  local copies, waits for them, and re-layouts  5.21 us (21%)
    pallas_call x1, Pallas kernels, per_device(): pl.pallas_call(functools.partial(kernel, (n_dom, n_sub)), out_shape=jax.S...  19.8 us
    unnamed x23, local copies, waits for them, and re-layouts  4.45 us
    pallas_call x1, local copies, waits for them, and re-layouts, per_device(): pl.pallas_call(functools.partial(kernel, (n_dom, n_sub)), out_shape=jax.S...  0.76 us

profile of v1, /device:TPU:0, one launch (start us, length us, event | category | flops | bytes accessed | tf_op | source)
XLA Modules:
  0.0 25.1 jit_solution(9406750998624896897)
XLA Ops:
  0.0 0.8 %copy.13.projection = f32[4,21,56]{2,1,0:T(8,128)S(1)} copy(f32[4,21,56]{2,0,1:T(4,128)} %param.13) | data formatting | bytes 37632 | tf_op args[2]
  0.8 0.0 copy-start.8
  0.8 1.0 %copy.14.star = f32[3,9,9,16]{3,2,1,0:T(8,128)S(1)} copy(f32[3,9,9,16]{3,0,2,1:T(4,128)} %param.14) | data formatting | bytes 31104 | tf_op args[3]
  1.8 0.0 copy-done.8
  1.8 0.0 copy-start.6
  1.8 0.1 copy.12.dofs
  1.9 0.8 %copy-done.6 = f32[4,9,9,16]{3,0,2,1:T(4,128)S(1)} copy-done((f32[4,9,9,16]{3,0,2,1:T(4,128)S(1)}, f32[4,9,9,16]{3,0,2,1:T(4,128)}, u32[]{:S(2)}) %copy-start.6) | copy-done | bytes 20760
  2.7 0.0 copy-start.7
  2.7 0.9 %copy-done.7 = f32[4,9,9,16]{3,0,2,1:T(4,128)S(1)} copy-done((f32[4,9,9,16]{3,0,2,1:T(4,128)S(1)}, f32[4,9,9,16]{3,0,2,1:T(4,128)}, u32[]{:S(2)}) %copy-start.7) | copy-done | bytes 20760
  3.6 0.0 copy-start
  3.6 0.0 copy-start.1
  3.6 0.0 copy-start.2
  3.6 0.0 copy-start.3
  3.6 0.0 copy-start.4
  3.6 0.0 copy-start.5
  3.7 0.8 %copy-done = f32[3,56,56]{2,1,0:T(8,128)S(1)} copy-done((f32[3,56,56]{2,1,0:T(8,128)S(1)}, f32[3,56,56]{2,1,0:T(8,128)}, u32[]{:S(2)}) %copy-start) | copy-done | bytes 37656
  4.5 0.0 copy-done.1
  4.5 0.0 copy-done.2
  4.5 0.0 copy-done.3
  4.5 0.0 copy-done.4
  4.5 0.0 copy-done.5
  4.5 19.8 %window.1 = f32[9,56,16]{2,1,0:T(8,128)S(1)} custom-call(f32[9,56,16]{2,1,0:T(8,128)S(1)} %copy.12.dofs, f32[3,56,56]{2,1,0:T(8,128)S(1)} %copy-done, f32[4,21,56]{2,1,0:T(8,128)S(1)} %copy.13.projection, f32[3,9,9,16]{3,2,1,0:T(8,128)S(1)} %copy.14.star, f32[4,9,9,16]{3,2,1,0:T(8,128)S(1)} %copy.15.flux_minus, f32[4,9,9,16]{3,2,1,0:T(8,128)S(1)} %copy.16.flux_plus, ...), custom_call_target="tpu_custom_call" | custom-call | tf_op jit(solution)/shard_map/window/pallas_call | solution.py:337
  24.3 0.8 %copy.17 = f32[9,56,16]{1,2,0:T(8,128)} copy(f32[9,56,16]{2,1,0:T(8,128)S(1)} %window.1) | data formatting | bytes 64512 | tf_op jit(solution)/shard_map/window/pallas_call | solution.py:337
  (2 shorter events, 0.1 us)
Async XLA Ops:
  0.8 1.0 %copy-start.8 = (f32[9,56,16]{1,2,0:T(8,128)S(1)}, f32[9,56,16]{1,2,0:T(8,128)}, u32[]{:S(2)}) copy-start(f32[9,56,16]{1,2,0:T(8,128)} %param.11) | copy-start | bytes 96772
  1.8 0.9 %copy-start.6 = (f32[4,9,9,16]{3,0,2,1:T(4,128)S(1)}, f32[4,9,9,16]{3,0,2,1:T(4,128)}, u32[]{:S(2)}) copy-start(f32[4,9,9,16]{3,0,2,1:T(4,128)} %param.15) | copy-start | bytes 62212
  2.7 0.9 %copy-start.7 = (f32[4,9,9,16]{3,0,2,1:T(4,128)S(1)}, f32[4,9,9,16]{3,0,2,1:T(4,128)}, u32[]{:S(2)}) copy-start(f32[4,9,9,16]{3,0,2,1:T(4,128)} %param.16) | copy-start | bytes 62212
  3.6 0.9 %copy-start = (f32[3,56,56]{2,1,0:T(8,128)S(1)}, f32[3,56,56]{2,1,0:T(8,128)}, u32[]{:S(2)}) copy-start(f32[3,56,56]{2,1,0:T(8,128)} %stiffness.1) | copy-start | bytes 112900
  3.6 0.9 %copy-start.1 = (f32[9,9]{1,0:T(8,128)S(1)}, f32[9,9]{1,0:T(8,128)}, u32[]{:S(2)}) copy-start(f32[9,9]{1,0:T(8,128)} %fault_flux.1) | copy-start | bytes 976
  3.6 0.9 %copy-start.2 = (s32[4,16]{1,0:T(4,128)S(1)}, s32[4,16]{1,0:T(4,128)}, u32[]{:S(2)}) copy-start(s32[4,16]{1,0:T(4,128)} %fault_faces.1) | copy-start | bytes 772
  3.6 0.9 %copy-start.3 = (s32[4,16]{1,0:T(4,128)S(1)}, s32[4,16]{1,0:T(4,128)}, u32[]{:S(2)}) copy-start(s32[4,16]{1,0:T(4,128)} %face_source.1) | copy-start | bytes 772
  3.6 0.9 %copy-start.4 = (s32[16]{0:T(128)S(1)}, s32[16]{0:T(128)}, u32[]{:S(2)}) copy-start(s32[16]{0:T(128)} %param.19) | copy-start | bytes 196
  3.6 0.9 %copy-start.5 = (s32[4]{0:T(128)S(1)}, s32[4]{0:T(128)}, u32[]{:S(2)}) copy-start(s32[4]{0:T(128)} %param.21) | copy-start | bytes 52

commit v2 on v1

v2 whole, which is shorter than its diff:
```python
import functools
import math

import jax
import jax.numpy as jnp
from jax import lax
from jax.experimental import pallas as pl
from jax.experimental.pallas import tpu as pltpu
from jax.sharding import PartitionSpec as P

MESH = pl.DeviceIdType.MESH
ORDER = 6
fine_step = 0.75
F32 = jnp.float32
BF16 = jnp.bfloat16


def taylor_weights(start_time, stop_time, term_count):
    return [
        (stop_time ** (term + 1) - start_time ** (term + 1)) / math.factorial(term + 1)
        for term in range(term_count)
    ]


def up_to(value, step):
    return -(-value // step) * step


def dot(a, b):
    return jnp.dot(a, b, preferred_element_type=F32)


def split(value):
    high = value.astype(BF16)
    return high, (value - high.astype(F32)).astype(BF16)


def stacked(value):
    return jnp.concatenate(split(value), axis=0)


def halves(product):
    rows = product.shape[0] // 2
    return product[:rows] + product[rows:]


def left_product(left_both, right):
    high, low = split(right)
    rows = left_both.shape[0] // 2
    return halves(dot(left_both, high)) + dot(left_both[:rows], low)


def right_product(left_both, right_high, right_low):
    rows = left_both.shape[0] // 2
    return halves(dot(left_both, right_high)) + dot(left_both[:rows], right_low)


def kernel(
    sizes,
    dofs_hbm,
    stiffness_hbm,
    projection_hbm,
    star_hbm,
    minus_hbm,
    plus_hbm,
    fault_hbm,
    fault_faces,
    levels,
    face_source,
    send_source,
    out,
    dofs,
    stiffness,
    projection,
    star,
    flux_minus,
    flux_plus,
    fault_flux,
    star_rows,
    minus_rows,
    plus_rows,
    fault_rows,
    ints,
    block_high,
    block_low,
    picks,
    send_picks,
    remote_picks,
    flat,
    small,
    turn_ref,
    export,
    received,
    table_ref,
    load_sem,
    send_sem,
    recv_sem,
):
    n_dom, n_sub = sizes
    var_count, elems, modes = dofs.shape
    dims = stiffness.shape[0]
    face_modes, faces = projection.shape[0], projection.shape[1]
    slots = send_source.shape[1]
    lanes = var_count * elems
    m_pad = up_to(modes, 16)
    j_pad = up_to(face_modes, 16)
    groups = up_to(face_modes, 8) // 8
    width = var_count * slots
    sources = 3 * n_sub
    tables, _, table_lanes = table_ref.shape
    per_table = table_lanes // width

    loads = [
        pltpu.make_async_copy(src, dst, load_sem.at[i])
        for i, (src, dst) in enumerate(
            (
                (star_hbm, star),
                (dofs_hbm, dofs),
                (stiffness_hbm, stiffness),
                (projection_hbm, projection),
                (fault_hbm, fault_flux),
                (minus_hbm, flux_minus),
                (plus_hbm, flux_plus),
            )
        )
    ]
    for load in loads:
        load.start()

    me_dom, me_sub = lax.axis_index("dom"), lax.axis_index("sub")
    partners = []
    for delta in (-1, 0, 1):
        for turn in range(n_sub):
            if delta or turn:
                partners.append(
                    (
                        (
                            lax.rem(me_dom + delta + n_dom, n_dom),
                            lax.rem(me_sub + turn, n_sub),
                        ),
                        (1 - delta) * n_sub + me_sub,
                    )
                )
    barrier = pltpu.get_barrier_semaphore()
    for target, _ in partners:
        pl.semaphore_signal(barrier, inc=1, device_id=target, device_id_type=MESH)

    small[...] = jnp.zeros_like(small)
    flat[...] = jnp.zeros_like(flat)
    turn_ref[...] = jnp.zeros_like(turn_ref)
    table_ref[...] = jnp.zeros_like(table_ref)
    export[...] = jnp.zeros_like(export)

    mask = (
        lax.broadcasted_iota(jnp.int32, (elems, lanes), 1) % elems
        == lax.broadcasted_iota(jnp.int32, (elems, lanes), 0)
    )

    def spread(rows, f, i):
        for w in range(var_count):
            row = rows[w, f : f + 1, :]
            high = row.astype(BF16).astype(F32)
            low = row - high
            at = slice(w * elems, (w + 1) * elems)
            block_high[i, at, :] = jnp.where(mask, high, 0.0).astype(BF16)
            block_low[i, at, :] = jnp.where(mask, low, 0.0).astype(BF16)

    loads[0].wait()
    for v in range(var_count):
        star_rows[:, :, v * elems : (v + 1) * elems] = star[v]
    for d in range(dims):
        spread(star_rows, d, d)

    loads[1].wait()
    turn_ref[0:lanes, 0:modes] = dofs[...].reshape(lanes, modes)
    state = jnp.transpose(turn_ref[...])[0:m_pad, 0:lanes]

    loads[2].wait()
    for d in range(dims):
        small[0:modes, d * m_pad : d * m_pad + modes] = stiffness[d]
    forward = stacked(small[0:m_pad, 0 : dims * m_pad])

    def turned(value):
        both = stacked(value)
        return [
            right_product(both, block_high[d], block_low[d]) for d in range(dims)
        ]

    def series(value, weight_sets):
        totals = [weights[0] * value for weights in weight_sets]
        for term in range(1, ORDER):
            value = left_product(forward, jnp.concatenate(turned(value), axis=0))
            totals = [
                total + weights[term] * value
                for total, weights in zip(totals, weight_sets)
            ]
        return totals

    first_weights = taylor_weights(0.0, fine_step, ORDER)
    second_weights = taylor_weights(fine_step, 2.0 * fine_step, ORDER)

    loads[3].wait()
    loads[4].wait()
    for d in range(dims):
        flat[d * m_pad : d * m_pad + modes, 0:modes] = stiffness[d]
    base = dims * m_pad
    for f in range(faces):
        flat[base + f * j_pad : base + f * j_pad + face_modes, 0:modes] = -projection[
            :, f, :
        ]
    base_fault = base + faces * j_pad
    flat[base_fault : base_fault + var_count, 0:var_count] = fault_flux[...]

    send_row = send_source[...]
    for i in range(width // slots):
        ints[9:10, i * slots : (i + 1) * slots] = send_row
    for v in range(var_count):
        at = slice(v * elems, (v + 1) * elems)
        ints[0:faces, at] = face_source[...]
        ints[4 : 4 + faces, at] = fault_faces[...]
        ints[8:9, at] = levels[...]

    def code(shape, dim, element_count):
        index = lax.broadcasted_iota(jnp.int32, shape, dim)
        return index // element_count, index % element_count

    row_var, row_elem = code((lanes, width), 0, elems)
    lane_var, _ = code((lanes, width), 1, slots)
    send_key = jnp.where(row_var == lane_var, row_elem, -(2**20))
    for f in range(faces):
        send_picks[f] = jnp.where(
            send_key == ints[9:10, 0:width] - f * elems, 1.0, 0.0
        ).astype(BF16)

    first_half, second_half = series(state, (first_weights, second_weights))

    project = stacked(-flat[base : base + faces * j_pad, 0:m_pad])
    flipped = jnp.transpose(flat[...])
    back = stacked(flipped[0:m_pad, 0:base_fault])

    def face_halves(value):
        both = stacked(left_product(project, value))
        count = faces * j_pad
        return [
            jnp.concatenate(
                [
                    both[f * j_pad : (f + 1) * j_pad],
                    both[count + f * j_pad : count + (f + 1) * j_pad],
                ],
                axis=0,
            )
            for f in range(faces)
        ]

    def total_of(parts):
        return functools.reduce(lambda a, b: a + b, parts)

    own_slot = n_sub + me_sub

    def launch(phase, face_parts):
        block = halves(
            total_of([dot(face_parts[f], send_picks[f]) for f in range(faces)])
        )
        for g in range(groups):
            export[phase, :, g * width : (g + 1) * width] = block[8 * g : 8 * g + 8]
        copies = []
        for i, (target, slot) in enumerate(partners):
            copy = pltpu.make_async_remote_copy(
                src_ref=export.at[phase],
                dst_ref=received.at[phase, slot],
                send_sem=send_sem.at[phase, i],
                recv_sem=recv_sem.at[phase, i],
                device_id=target,
                device_id_type=MESH,
            )
            copy.start()
            copies.append(copy)
        received[phase, own_slot] = export[phase]
        return copies

    def local_part(value, face_parts):
        volume = turned(value)
        own = [
            right_product(face_parts[f], block_high[dims + f], block_low[dims + f])
            for f in range(faces)
        ]
        beside = [
            total_of([dot(face_parts[g], picks[g, f]) for g in range(faces)])
            for f in range(faces)
        ]
        return volume, own, beside

    def finish(phase, copies, parts):
        volume, own, beside = parts
        for copy in copies:
            copy.wait()
        for k in range(sources):
            t, at = k // per_table, k % per_table * width
            for g in range(groups):
                table_ref[t, 8 * g : 8 * g + 8, at : at + width] = received[
                    phase, k, :, g * width : (g + 1) * width
                ]
        table_parts = [stacked(table_ref[t]) for t in range(tables)]
        flux = []
        for f in range(faces):
            gathered = halves(
                beside[f]
                + total_of([dot(table_parts[t], remote_picks[t, f]) for t in range(tables)])
            )
            at = dims + faces + f
            flux.append(
                own[f] + right_product(stacked(gathered), block_high[at], block_low[at])
            )
        return left_product(back, jnp.concatenate(volume + flux, axis=0))

    face_parts = face_halves(first_half)
    pl.semaphore_wait(barrier, len(partners))
    copies = launch(0, face_parts)

    loads[5].wait()
    loads[6].wait()
    for v in range(var_count):
        at = slice(v * elems, (v + 1) * elems)
        minus_rows[:, :, at] = flux_minus[v]
        plus_rows[:, :, at] = flux_plus[v]
        fault_rows[0:var_count, at] = jnp.broadcast_to(
            flipped[0:var_count, base_fault + v : base_fault + v + 1], (var_count, elems)
        )
    on_fault = ints[4 : 4 + faces, :] == 1
    for w in range(var_count):
        plus_rows[w] = jnp.where(on_fault, fault_rows[w : w + 1, :], plus_rows[w])
    for f in range(faces):
        spread(minus_rows, f, dims + f)
        spread(plus_rows, f, dims + faces + f)
    row_var, row_elem = code((lanes, lanes), 0, elems)
    lane_var, _ = code((lanes, lanes), 1, elems)
    key = jnp.where(row_var == lane_var, row_elem, -(2**20))
    source_id, inside = code((table_lanes, lanes), 0, width)
    slot_var, slot = inside // slots, inside % slots
    lane_var, _ = code((table_lanes, lanes), 1, elems)
    remote_key = jnp.where(
        slot_var == lane_var, faces * elems + source_id * slots + slot, -(2**20)
    )
    for f in range(faces):
        wanted = ints[f : f + 1, :]
        for g in range(faces):
            picks[g, f] = jnp.where(key == wanted - g * elems, 1.0, 0.0).astype(BF16)
        for t in range(tables):
            remote_picks[t, f] = jnp.where(
                remote_key == wanted - t * per_table * slots, 1.0, 0.0
            ).astype(BF16)

    parts = local_part(first_half, face_parts)
    moved = state + finish(0, copies, parts)
    (fine_half,) = series(moved, (first_weights,))
    carried = jnp.where(ints[8:9, :] == 0, fine_half, second_half)
    face_parts = face_halves(carried)
    copies = launch(1, face_parts)
    parts = local_part(carried, face_parts)
    result = moved + finish(1, copies, parts)
    turned_back = jnp.transpose(
        jnp.concatenate(
            [
                jnp.concatenate(
                    [result, jnp.zeros((m_pad, turn_ref.shape[0] - lanes), F32)], axis=1
                ),
                jnp.zeros((128 - m_pad, turn_ref.shape[0]), F32),
            ],
            axis=0,
        )
    )
    out[...] = turned_back[0:lanes, 0:modes].reshape(var_count, elems, modes)


def solution(mesh):
    n_dom, n_sub = mesh.shape["dom"], mesh.shape["sub"]

    def per_device(
        dofs,
        stiffness,
        projection,
        star,
        flux_minus,
        flux_plus,
        fault_flux,
        fault_faces,
        levels,
        face_source,
        send_source,
    ):
        var_count, modes, elems = dofs.shape
        dims = stiffness.shape[0]
        faces, face_modes = projection.shape[0], projection.shape[1]
        slots = send_source.shape[0]
        lanes = var_count * elems
        m_pad, j_pad = up_to(modes, 16), up_to(face_modes, 16)
        width = var_count * slots
        sources = 3 * n_sub
        tables = -(-sources // (256 // width))
        per_table = -(-sources // tables)
        blocks = dims + 2 * faces
        flat_rows = up_to(dims * m_pad + faces * j_pad + var_count, 128)
        vmem = pl.BlockSpec(memory_space=pltpu.VMEM)
        whole = pl.BlockSpec(memory_space=pltpu.HBM)
        moved = [
            jnp.transpose(dofs, (0, 2, 1)),
            stiffness,
            jnp.transpose(projection, (1, 0, 2)),
            jnp.transpose(star, (1, 2, 0, 3)),
            jnp.transpose(flux_minus, (1, 2, 0, 3)),
            jnp.transpose(flux_plus, (1, 2, 0, 3)),
            fault_flux,
        ]
        result = pl.pallas_call(
            functools.partial(kernel, (n_dom, n_sub)),
            out_shape=jax.ShapeDtypeStruct((var_count, elems, modes), F32),
            in_specs=[whole] * 7 + [vmem] * 4,
            out_specs=vmem,
            scratch_shapes=[pltpu.VMEM(one.shape, F32) for one in moved]
            + [
                pltpu.VMEM((var_count, dims, lanes), F32),
                pltpu.VMEM((var_count, faces, lanes), F32),
                pltpu.VMEM((var_count, faces, lanes), F32),
                pltpu.VMEM((up_to(var_count, 8), lanes), F32),
                pltpu.VMEM((16, lanes), jnp.int32),
                pltpu.VMEM((blocks, lanes, lanes), BF16),
                pltpu.VMEM((blocks, lanes, lanes), BF16),
                pltpu.VMEM((faces, faces, lanes, lanes), BF16),
                pltpu.VMEM((faces, lanes, width), BF16),
                pltpu.VMEM((tables, faces, per_table * width, lanes), BF16),
                pltpu.VMEM((flat_rows, 128), F32),
                pltpu.VMEM((m_pad, up_to(dims * m_pad, 128)), F32),
                pltpu.VMEM((up_to(lanes, 128), 128), F32),
                pltpu.VMEM((2, 8, 128), F32),
                pltpu.VMEM((2, sources, 8, 128), F32),
                pltpu.VMEM((tables, j_pad, per_table * width), F32),
                pltpu.SemaphoreType.DMA((len(moved),)),
                pltpu.SemaphoreType.DMA((2, sources - 1)),
                pltpu.SemaphoreType.DMA((2, sources - 1)),
            ],
            compiler_params=pltpu.CompilerParams(
                collective_id=0,
                has_side_effects=True,
                vmem_limit_bytes=48 * 1024 * 1024,
            ),
            name="window",
        )(
            *moved,
            fault_faces,
            levels.reshape(1, -1),
            face_source,
            send_source.reshape(1, -1),
        )
        return jnp.transpose(result, (0, 2, 1))

    return jax.shard_map(
        per_device,
        mesh=mesh,
        in_specs=(
            P(None, None, ("dom", "sub")),
            P(),
            P(),
            P(None, None, None, ("dom", "sub")),
            P(None, None, None, ("dom", "sub")),
            P(None, None, None, ("dom", "sub")),
            P(),
            P(None, ("dom", "sub")),
            P(("dom", "sub")),
            P(None, ("dom", "sub")),
            P(("dom", "sub")),
        ),
        out_specs=P(None, None, ("dom", "sub")),
        check_vma=False,
    )
```

time: 25.3 us -> 26.8 us (1.059)
  local copies, waits for them, and re-layouts: 5.21 us -> 6.65 us
    unnamed x23, local copies, waits for them, and re-layouts: 4.45 us -> 6.65 us
    pallas_call x1 -> x0, local copies, waits for them, and re-layouts: 0.76 us -> none  [per_device(): pl.pallas_call(functools.partial(kernel, (n_dom, n_sub)), out_shape=jax.S...]
where the time goes in v2:
time: 26.8 us; the launch traced here: 26.5 us
  Pallas kernels  19.8 us (74%)
  local copies, waits for them, and re-layouts  6.65 us (25%)
    pallas_call x1, Pallas kernels, per_device(): pl.pallas_call(functools.partial(kernel, (n_dom, n_sub)), out_shape=jax.S...  19.8 us
    unnamed x23, local copies, waits for them, and re-layouts  6.65 us

profile of v2, /device:TPU:0, one launch (start us, length us, event | category | flops | bytes accessed | tf_op | source)
XLA Modules:
  0.0 26.5 jit_solution(13057548731906518169)
XLA Ops:
  0.0 0.0 copy-start.6
  0.0 0.0 copy-start.8
  0.0 0.0 copy-start.7
  0.0 0.0 copy-start.9
  0.0 0.0 copy-start.10
  0.0 0.7 %copy-done.6 = f32[9,9]{1,0:T(8,128)S(1)} copy-done((f32[9,9]{1,0:T(8,128)S(1)}, f32[9,9]{1,0:T(8,128)}, u32[]{:S(2)}) %copy-start.6) | copy-done | bytes 348
  0.7 0.0 copy-done.8
  0.7 0.0 copy-done.7
  0.7 0.0 copy-done.9
  0.7 0.0 copy-done.10
  0.7 0.0 copy-start
  0.7 0.9 %copy-done = f32[3,9,9,16]{3,0,2,1:T(4,128)S(1)} copy-done((f32[3,9,9,16]{3,0,2,1:T(4,128)S(1)}, f32[3,9,9,16]{3,0,2,1:T(4,128)}, u32[]{:S(2)}) %copy-start) | copy-done | bytes 15576
  1.6 0.0 copy-start.1
  1.6 0.9 %copy-done.1 = f32[4,9,9,16]{3,0,2,1:T(4,128)S(1)} copy-done((f32[4,9,9,16]{3,0,2,1:T(4,128)S(1)}, f32[4,9,9,16]{3,0,2,1:T(4,128)}, u32[]{:S(2)}) %copy-start.1) | copy-done | bytes 20760
  2.6 0.0 copy-start.2
  2.6 0.9 %copy-done.2 = f32[4,9,9,16]{3,0,2,1:T(4,128)S(1)} copy-done((f32[4,9,9,16]{3,0,2,1:T(4,128)S(1)}, f32[4,9,9,16]{3,0,2,1:T(4,128)}, u32[]{:S(2)}) %copy-start.2) | copy-done | bytes 20760
  3.5 0.0 copy-start.3
  3.5 0.9 %copy-done.3 = f32[3,56,56]{2,1,0:T(8,128)S(1)} copy-done((f32[3,56,56]{2,1,0:T(8,128)S(1)}, f32[3,56,56]{2,1,0:T(8,128)}, u32[]{:S(2)}) %copy-start.3) | copy-done | bytes 37656
  4.4 0.0 copy-start.4
  4.4 0.9 %copy-done.4 = f32[9,56,16]{1,2,0:T(8,128)S(1)} copy-done((f32[9,56,16]{1,2,0:T(8,128)S(1)}, f32[9,56,16]{1,2,0:T(8,128)}, u32[]{:S(2)}) %copy-start.4) | copy-done | bytes 32280
  5.2 0.0 copy-start.5
  5.2 0.8 %copy-done.5 = f32[4,21,56]{2,0,1:T(4,128)S(1)} copy-done((f32[4,21,56]{2,0,1:T(4,128)S(1)}, f32[4,21,56]{2,0,1:T(4,128)}, u32[]{:S(2)}) %copy-start.5) | copy-done | bytes 18840
  6.0 19.8 %window.1 = f32[9,16,56]{2,1,0:T(8,128)S(1)} custom-call(f32[9,16,56]{2,1,0:T(8,128)S(1)} %bitcast.12, f32[3,56,56]{2,1,0:T(8,128)S(1)} %copy-done.3, f32[21,4,56]{2,1,0:T(4,128)S(1)} %bitcast.13, f32[9,9,3,16]{3,2,1,0:T(4,128)S(1)} %bitcast.9, f32[9,9,4,16]{3,2,1,0:T(4,128)S(1)} %bitcast.10, f32[9,9,4,16]{3,2,1,0:T(4,128)S(1)} %bitcast.11, ...), custom_call_target="tpu_custom_call" | custom-call | tf_op jit(solution)/shard_map/window/pallas_call | solution.py:414
  25.9 0.6 %copy.13 = f32[9,56,16]{1,2,0:T(8,128)} copy(f32[9,56,16]{1,2,0:T(8,128)S(1)} %bitcast.8) | data formatting | bytes 64512
Async XLA Ops:
  0.0 0.7 %copy-start.6 = (f32[9,9]{1,0:T(8,128)S(1)}, f32[9,9]{1,0:T(8,128)}, u32[]{:S(2)}) copy-start(f32[9,9]{1,0:T(8,128)} %fault_hbm.1) | copy-start | bytes 976
  0.0 0.7 %copy-start.8 = (s32[4,16]{1,0:T(4,128)S(1)}, s32[4,16]{1,0:T(4,128)}, u32[]{:S(2)}) copy-start(s32[4,16]{1,0:T(4,128)} %face_source.1) | copy-start | bytes 772
  0.0 0.7 %copy-start.7 = (s32[4,16]{1,0:T(4,128)S(1)}, s32[4,16]{1,0:T(4,128)}, u32[]{:S(2)}) copy-start(s32[4,16]{1,0:T(4,128)} %fault_faces.1) | copy-start | bytes 772
  0.0 0.7 %copy-start.9 = (s32[16]{0:T(128)S(1)}, s32[16]{0:T(128)}, u32[]{:S(2)}) copy-start(s32[16]{0:T(128)} %param.19) | copy-start | bytes 196
  0.0 0.7 %copy-start.10 = (s32[4]{0:T(128)S(1)}, s32[4]{0:T(128)}, u32[]{:S(2)}) copy-start(s32[4]{0:T(128)} %param.21) | copy-start | bytes 52
  0.7 0.9 %copy-start = (f32[3,9,9,16]{3,0,2,1:T(4,128)S(1)}, f32[3,9,9,16]{3,0,2,1:T(4,128)}, u32[]{:S(2)}) copy-start(f32[3,9,9,16]{3,0,2,1:T(4,128)} %param.14) | copy-start | bytes 46660
  1.6 0.9 %copy-start.1 = (f32[4,9,9,16]{3,0,2,1:T(4,128)S(1)}, f32[4,9,9,16]{3,0,2,1:T(4,128)}, u32[]{:S(2)}) copy-start(f32[4,9,9,16]{3,0,2,1:T(4,128)} %param.15) | copy-start | bytes 62212
  2.6 0.9 %copy-start.2 = (f32[4,9,9,16]{3,0,2,1:T(4,128)S(1)}, f32[4,9,9,16]{3,0,2,1:T(4,128)}, u32[]{:S(2)}) copy-start(f32[4,9,9,16]{3,0,2,1:T(4,128)} %param.16) | copy-start | bytes 62212
  3.5 0.9 %copy-start.3 = (f32[3,56,56]{2,1,0:T(8,128)S(1)}, f32[3,56,56]{2,1,0:T(8,128)}, u32[]{:S(2)}) copy-start(f32[3,56,56]{2,1,0:T(8,128)} %stiffness_hbm.1) | copy-start | bytes 112900
  4.4 0.9 %copy-start.4 = (f32[9,56,16]{1,2,0:T(8,128)S(1)}, f32[9,56,16]{1,2,0:T(8,128)}, u32[]{:S(2)}) copy-start(f32[9,56,16]{1,2,0:T(8,128)} %param.11) | copy-start | bytes 96772
  5.2 0.8 %copy-start.5 = (f32[4,21,56]{2,0,1:T(4,128)S(1)}, f32[4,21,56]{2,0,1:T(4,128)}, u32[]{:S(2)}) copy-start(f32[4,21,56]{2,0,1:T(4,128)} %param.13) | copy-start | bytes 56452

commit v3 on v2

--- a/solution.py
+++ b/solution.py
@@ -441,7 +441,7 @@
             compiler_params=pltpu.CompilerParams(
                 collective_id=0,
                 has_side_effects=True,
-                vmem_limit_bytes=48 * 1024 * 1024,
+                vmem_limit_bytes=67_043_328,
             ),
             name="window",
         )(

time: 26.8 us -> 22.1 us (0.82)
  local copies, waits for them, and re-layouts: 6.65 us -> 1.52 us
  Pallas kernels: 19.8 us -> 20.4 us
    unnamed x23 -> x1, local copies, waits for them, and re-layouts: 6.65 us -> 1.52 us
    pallas_call x1, Pallas kernels: 19.8 us -> 20.4 us  [per_device(): pl.pallas_call(functools.partial(kernel, (n_dom, n_sub)), out_shape=jax.S...]
where the time goes in v3:
time: 22.1 us; the launch traced here: 21.9 us
  Pallas kernels  20.4 us (92%)
  local copies, waits for them, and re-layouts  1.52 us (7%)
    pallas_call x1, Pallas kernels, per_device(): pl.pallas_call(functools.partial(kernel, (n_dom, n_sub)), out_shape=jax.S...  20.4 us
    unnamed x1, local copies, waits for them, and re-layouts  1.52 us

profile of v3, /device:TPU:0, one launch (start us, length us, event | category | flops | bytes accessed | tf_op | source)
XLA Modules:
  0.0 21.9 jit_solution(2253470933301324849)
XLA Ops:
  0.0 20.4 %window.1 = f32[9,16,56]{2,1,0:T(8,128)} custom-call(f32[9,16,56]{2,1,0:T(8,128)} %bitcast.12, f32[3,56,56]{2,1,0:T(8,128)} %stiffness_hbm.1, f32[21,4,56]{2,1,0:T(4,128)} %bitcast.13, f32[9,9,3,16]{3,2,1,0:T(4,128)} %bitcast.9, f32[9,9,4,16]{3,2,1,0:T(4,128)} %bitcast.10, f32[9,9,4,16]{3,2,1,0:T(4,128)} %bitcast.11, f32[9,9]{1,0:T(8,128)} %fault_hbm.1, ...), custom_call_target="tpu_custom_call" | custom-call | tf_op jit(solution)/shard_map/window/pallas_call | solution.py:414
  20.4 1.5 %copy.13 = f32[9,56,16]{1,2,0:T(8,128)} copy(f32[9,56,16]{1,2,0:T(8,128)} %bitcast.8) | data formatting | bytes 64512

commit v4 on v3

--- a/solution.py
+++ b/solution.py
@@ -165,6 +165,45 @@
             block_high[i, at, :] = jnp.where(mask, high, 0.0).astype(BF16)
             block_low[i, at, :] = jnp.where(mask, low, 0.0).astype(BF16)
 
+    send_row = send_source[...]
+    for i in range(width // slots):
+        ints[9:10, i * slots : (i + 1) * slots] = send_row
+    for v in range(var_count):
+        at = slice(v * elems, (v + 1) * elems)
+        ints[0:faces, at] = face_source[...]
+        ints[4 : 4 + faces, at] = fault_faces[...]
+        ints[8:9, at] = levels[...]
+
+    def code(shape, dim, element_count):
+        index = lax.broadcasted_iota(jnp.int32, shape, dim)
+        return index // element_count, index % element_count
+
+    row_var, row_elem = code((lanes, width), 0, elems)
+    lane_var, _ = code((lanes, width), 1, slots)
+    send_key = jnp.where(row_var == lane_var, row_elem, -(2**20))
+    for f in range(faces):
+        send_picks[f] = jnp.where(
+            send_key == ints[9:10, 0:width] - f * elems, 1.0, 0.0
+        ).astype(BF16)
+
+    row_var, row_elem = code((lanes, lanes), 0, elems)
+    lane_var, _ = code((lanes, lanes), 1, elems)
+    key = jnp.where(row_var == lane_var, row_elem, -(2**20))
+    source_id, inside = code((table_lanes, lanes), 0, width)
+    slot_var, slot = inside // slots, inside % slots
+    lane_var, _ = code((table_lanes, lanes), 1, elems)
+    remote_key = jnp.where(
+        slot_var == lane_var, faces * elems + source_id * slots + slot, -(2**20)
+    )
+    for f in range(faces):
+        wanted = ints[f : f + 1, :]
+        for g in range(faces):
+            picks[g, f] = jnp.where(key == wanted - g * elems, 1.0, 0.0).astype(BF16)
+        for t in range(tables):
+            remote_picks[t, f] = jnp.where(
+                remote_key == wanted - t * per_table * slots, 1.0, 0.0
+            ).astype(BF16)
+
     loads[0].wait()
     for v in range(var_count):
         star_rows[:, :, v * elems : (v + 1) * elems] = star[v]
@@ -211,32 +250,9 @@
     base_fault = base + faces * j_pad
     flat[base_fault : base_fault + var_count, 0:var_count] = fault_flux[...]
 
-    send_row = send_source[...]
-    for i in range(width // slots):
-        ints[9:10, i * slots : (i + 1) * slots] = send_row
-    for v in range(var_count):
-        at = slice(v * elems, (v + 1) * elems)
-        ints[0:faces, at] = face_source[...]
-        ints[4 : 4 + faces, at] = fault_faces[...]
-        ints[8:9, at] = levels[...]
-
-    def code(shape, dim, element_count):
-        index = lax.broadcasted_iota(jnp.int32, shape, dim)
-        return index // element_count, index % element_count
-
-    row_var, row_elem = code((lanes, width), 0, elems)
-    lane_var, _ = code((lanes, width), 1, slots)
-    send_key = jnp.where(row_var == lane_var, row_elem, -(2**20))
-    for f in range(faces):
-        send_picks[f] = jnp.where(
-            send_key == ints[9:10, 0:width] - f * elems, 1.0, 0.0
-        ).astype(BF16)
-
     first_half, second_half = series(state, (first_weights, second_weights))
 
     project = stacked(-flat[base : base + faces * j_pad, 0:m_pad])
-    flipped = jnp.transpose(flat[...])
-    back = stacked(flipped[0:m_pad, 0:base_fault])
 
     def face_halves(value):
         both = stacked(left_product(project, value))
@@ -290,10 +306,10 @@
         ]
         return volume, own, beside
 
-    def finish(phase, copies, parts):
+    def finish(phase, copies, parts, back):
         volume, own, beside = parts
         for copy in copies:
-            copy.wait()
+            copy.wait_recv()
         for k in range(sources):
             t, at = k // per_table, k % per_table * width
             for g in range(groups):
@@ -317,6 +333,8 @@
     pl.semaphore_wait(barrier, len(partners))
     copies = launch(0, face_parts)
 
+    flipped = jnp.transpose(flat[...])
+    back = stacked(flipped[0:m_pad, 0:base_fault])
     loads[5].wait()
     loads[6].wait()
     for v in range(var_count):
@@ -332,32 +350,14 @@
     for f in range(faces):
         spread(minus_rows, f, dims + f)
         spread(plus_rows, f, dims + faces + f)
-    row_var, row_elem = code((lanes, lanes), 0, elems)
-    lane_var, _ = code((lanes, lanes), 1, elems)
-    key = jnp.where(row_var == lane_var, row_elem, -(2**20))
-    source_id, inside = code((table_lanes, lanes), 0, width)
-    slot_var, slot = inside // slots, inside % slots
-    lane_var, _ = code((table_lanes, lanes), 1, elems)
-    remote_key = jnp.where(
-        slot_var == lane_var, faces * elems + source_id * slots + slot, -(2**20)
-    )
-    for f in range(faces):
-        wanted = ints[f : f + 1, :]
-        for g in range(faces):
-            picks[g, f] = jnp.where(key == wanted - g * elems, 1.0, 0.0).astype(BF16)
-        for t in range(tables):
-            remote_picks[t, f] = jnp.where(
-                remote_key == wanted - t * per_table * slots, 1.0, 0.0
-            ).astype(BF16)
-
     parts = local_part(first_half, face_parts)
-    moved = state + finish(0, copies, parts)
+    moved = state + finish(0, copies, parts, back)
     (fine_half,) = series(moved, (first_weights,))
     carried = jnp.where(ints[8:9, :] == 0, fine_half, second_half)
     face_parts = face_halves(carried)
-    copies = launch(1, face_parts)
+    last_copies = launch(1, face_parts)
     parts = local_part(carried, face_parts)
-    result = moved + finish(1, copies, parts)
+    result = moved + finish(1, last_copies, parts, back)
     turned_back = jnp.transpose(
         jnp.concatenate(
             [
@@ -370,6 +370,8 @@
         )
     )
     out[...] = turned_back[0:lanes, 0:modes].reshape(var_count, elems, modes)
+    for copy in copies + last_copies:
+        copy.wait_send()
 
 
 def solution(mesh):
@@ -413,7 +415,7 @@
         ]
         result = pl.pallas_call(
             functools.partial(kernel, (n_dom, n_sub)),
-            out_shape=jax.ShapeDtypeStruct((var_count, elems, modes), F32),
+            out_shape=pltpu.VMEM((var_count, elems, modes), F32),
             in_specs=[whole] * 7 + [vmem] * 4,
             out_specs=vmem,
             scratch_shapes=[pltpu.VMEM(one.shape, F32) for one in moved]
@@ -441,7 +443,7 @@
             compiler_params=pltpu.CompilerParams(
                 collective_id=0,
                 has_side_effects=True,
-                vmem_limit_bytes=67_043_328,
+                vmem_limit_bytes=66_000_000,
             ),
             name="window",
         )(

time: 22.1 us -> 20.6 us (0.932)
  local copies, waits for them, and re-layouts: 1.52 us -> 0.64 us
  Pallas kernels: 20.4 us -> 19.8 us
    unnamed x1, local copies, waits for them, and re-layouts: 1.52 us -> 0.64 us
    pallas_call x1, Pallas kernels: 20.4 us -> 19.8 us  [per_device(): pl.pallas_call(functools.partial(kernel, (n_dom, n_sub)), out_shape=pltpu...]
where the time goes in v4:
time: 20.6 us; the launch traced here: 20.4 us
  Pallas kernels  19.8 us (96%)
  local copies, waits for them, and re-layouts  0.64 us (3%)
    pallas_call x1, Pallas kernels, per_device(): pl.pallas_call(functools.partial(kernel, (n_dom, n_sub)), out_shape=pltpu...  19.8 us
    unnamed x1, local copies, waits for them, and re-layouts  0.64 us

profile of v4, /device:TPU:0, one launch (start us, length us, event | category | flops | bytes accessed | tf_op | source)
XLA Modules:
  0.0 20.4 jit_solution(303269296416127709)
XLA Ops:
  0.0 19.8 %window.1 = f32[9,16,56]{2,1,0:T(8,128)S(1)} custom-call(f32[9,16,56]{2,1,0:T(8,128)} %bitcast.12, f32[3,56,56]{2,1,0:T(8,128)} %stiffness_hbm.1, f32[21,4,56]{2,1,0:T(4,128)} %bitcast.13, f32[9,9,3,16]{3,2,1,0:T(4,128)} %bitcast.9, f32[9,9,4,16]{3,2,1,0:T(4,128)} %bitcast.10, f32[9,9,4,16]{3,2,1,0:T(4,128)} %bitcast.11, f32[9,9]{1,0:T(8,128)} %fault_hbm.1, ...), custom_call_target="tpu_custom_call" | custom-call | tf_op jit(solution)/shard_map/window/pallas_call | solution.py:416
  19.8 0.6 %copy.13 = f32[9,56,16]{1,2,0:T(8,128)} copy(f32[9,56,16]{1,2,0:T(8,128)S(1)} %bitcast.8) | data formatting | bytes 64512

commit v5 on v4

--- a/solution.py
+++ b/solution.py
@@ -294,7 +294,7 @@
         received[phase, own_slot] = export[phase]
         return copies
 
-    def local_part(value, face_parts):
+    def local_part(value, face_parts, back):
         volume = turned(value)
         own = [
             right_product(face_parts[f], block_high[dims + f], block_low[dims + f])
@@ -304,10 +304,18 @@
             total_of([dot(face_parts[g], picks[g, f]) for g in range(faces)])
             for f in range(faces)
         ]
-        return volume, own, beside
+        flux = [
+            own[f]
+            + right_product(
+                stacked(halves(beside[f])),
+                block_high[dims + faces + f],
+                block_low[dims + faces + f],
+            )
+            for f in range(faces)
+        ]
+        return left_product(back, jnp.concatenate(volume + flux, axis=0))
 
     def finish(phase, copies, parts, back):
-        volume, own, beside = parts
         for copy in copies:
             copy.wait_recv()
         for k in range(sources):
@@ -320,14 +328,13 @@
         flux = []
         for f in range(faces):
             gathered = halves(
-                beside[f]
-                + total_of([dot(table_parts[t], remote_picks[t, f]) for t in range(tables)])
+                total_of([dot(table_parts[t], remote_picks[t, f]) for t in range(tables)])
             )
             at = dims + faces + f
             flux.append(
-                own[f] + right_product(stacked(gathered), block_high[at], block_low[at])
-            )
-        return left_product(back, jnp.concatenate(volume + flux, axis=0))
+                right_product(stacked(gathered), block_high[at], block_low[at])
+            )
+        return parts + left_product(back[:, base:], jnp.concatenate(flux, axis=0))
 
     face_parts = face_halves(first_half)
     pl.semaphore_wait(barrier, len(partners))
@@ -350,13 +357,13 @@
     for f in range(faces):
         spread(minus_rows, f, dims + f)
         spread(plus_rows, f, dims + faces + f)
-    parts = local_part(first_half, face_parts)
+    parts = local_part(first_half, face_parts, back)
     moved = state + finish(0, copies, parts, back)
     (fine_half,) = series(moved, (first_weights,))
     carried = jnp.where(ints[8:9, :] == 0, fine_half, second_half)
     face_parts = face_halves(carried)
     last_copies = launch(1, face_parts)
-    parts = local_part(carried, face_parts)
+    parts = local_part(carried, face_parts, back)
     result = moved + finish(1, last_copies, parts, back)
     turned_back = jnp.transpose(
         jnp.concatenate(

time: 20.6 us -> 20.4 us (level)
  no operation moved by 1% of the time
where the time goes in v5:
time: 20.4 us; the launch traced here: 20.3 us
  Pallas kernels  19.6 us (96%)
  local copies, waits for them, and re-layouts  0.64 us (3%)
    pallas_call x1, Pallas kernels, per_device(): pl.pallas_call(functools.partial(kernel, (n_dom, n_sub)), out_shape=pltpu...  19.6 us
    unnamed x1, local copies, waits for them, and re-layouts  0.64 us

profile of v5, /device:TPU:0, one launch (start us, length us, event | category | flops | bytes accessed | tf_op | source)
XLA Modules:
  0.0 20.3 jit_solution(354411021869394839)
XLA Ops:
  0.0 19.6 %window.1 = f32[9,16,56]{2,1,0:T(8,128)S(1)} custom-call(f32[9,16,56]{2,1,0:T(8,128)} %bitcast.12, f32[3,56,56]{2,1,0:T(8,128)} %stiffness_hbm.1, f32[21,4,56]{2,1,0:T(4,128)} %bitcast.13, f32[9,9,3,16]{3,2,1,0:T(4,128)} %bitcast.9, f32[9,9,4,16]{3,2,1,0:T(4,128)} %bitcast.10, f32[9,9,4,16]{3,2,1,0:T(4,128)} %bitcast.11, f32[9,9]{1,0:T(8,128)} %fault_hbm.1, ...), custom_call_target="tpu_custom_call" | custom-call | tf_op jit(solution)/shard_map/window/pallas_call | solution.py:423
  19.6 0.6 %copy.13 = f32[9,56,16]{1,2,0:T(8,128)} copy(f32[9,56,16]{1,2,0:T(8,128)S(1)} %bitcast.8) | data formatting | bytes 64512
